TPU v7x, 128 devices: a whole 4x4x4 slice. The times are simulated.
128 devices in a mesh: span: 32 (over y, z, core), wall: 4 (over x).
Axes of the slice: x: 4, y: 4, z: 4, core: 2. Of those that a mesh axis runs over, the one named last changes fastest.
Arguments:
- random_field: float32 [3, 2048, 65536], P(None, 'wall', 'span'), may hold values from -6 to 6
- half_widths: int32 [2048], replicated, may hold values from 1 to 256, as said below
- band_pads: int32 [32], replicated, may hold values from 1 to 256, as said below
- span_widths: int32 [32], replicated, may hold values from 1 to 64, as said below
- stresses: float32 [6, 2048], P(None, 'wall'), as said below
- mean_flow: float32 [2048], P('wall'), may hold values from 0.3 to 1.2
Outputs:
- velocity: float32 [3, 2048, 65536], P(None, 'wall', 'span')
Inputs may be any that keep to these rules, and one draw needn't show every extreme that they name: `half_widths`: every row's value is at most the band_pads value of its band of 64 rows; some row reaches 256. `band_pads`: some band reaches 256. `span_widths`: some band reaches 64. `stresses`: each row's six entries form a positive definite tensor whose correlation coefficients are at most 0.4 in magnitude; the diagonal entries lie between 0.3 and 3.
All inputs are finite; a program needn't handle non-finite values.
Results may differ from a plain program's by a relative error of at most 0.0003.
Values sent between devices are 32-bit elements; how exact they have to be, the bound alone decides.
No kernel may reach another device: no remote copies, remote signals or barrier semaphores. Data moves between devices by JAX's collectives and lax.ppermute only.
A program may use at most 192 MiB of HBM per device.

v0:
```python
import functools

import jax
import jax.numpy as jnp
from jax import lax
from jax.experimental import pallas as pl
from jax.experimental.pallas import tpu as pltpu
from jax.sharding import PartitionSpec as P

MAXW = 256
SPMAX = 64
BAND = 64
REACH = 2 * SPMAX
TILE = 4 * SPMAX
SIZES = (152, 184, 256)


def split(values):
    high = values.astype(jnp.bfloat16)
    return high, (values - high.astype(jnp.float32)).astype(jnp.bfloat16)


def dot(left, right):
    return lax.dot_general(left, right, (((1,), (0,)), ((), ())), preferred_element_type=jnp.float32)


def dot3(left_high, left_low, right_high, right_low):
    return dot(left_high, right_high) + (dot(left_high, right_low) + dot(left_low, right_high))


def whole(array):
    return pl.BlockSpec(array.shape, lambda *_: (0,) * len(array.shape))


def iota(shape, axis):
    return lax.broadcasted_iota(jnp.int32, shape, axis).astype(jnp.float32)


def wall_coeff(distance, rate, pad, inverse):
    return jnp.where(distance <= pad, jnp.exp(distance * distance * rate) * inverse, 0.0)


def rate_of(width):
    return (-0.5 * jnp.pi) / (width * width)


def inverse_norm(width, pad):
    steps = iota((1, MAXW + 128), 1)
    profile = wall_coeff(steps, rate_of(width), pad, 1.0)
    return 1.0 / jnp.sqrt(2.0 * jnp.sum(profile * profile, axis=1, keepdims=True) - 1.0)


def cover(width, pad, depth):
    need = jnp.floor(jnp.minimum(pad, width * 8.25)) - depth
    counts = iota((1, MAXW + 128), 1)
    total = jnp.sum(jnp.where(need > counts, 1.0, 0.0), axis=0, keepdims=True) + counts
    key = jnp.min(jnp.where(counts <= MAXW, total, 4096.0) * 512.0 + counts, axis=1, keepdims=True)
    cost = jnp.floor(key * (1.0 / 512.0))
    best = key - cost * 512.0
    return need, best, cost


def slots(need, best):
    part = jnp.where(need > best, 1.0, 0.0)
    earlier = jnp.where(iota((MAXW, MAXW), 1) < iota((MAXW, MAXW), 0), 1.0, 0.0).astype(jnp.bfloat16)
    before = dot(earlier, jnp.broadcast_to(part, (MAXW, 128)).astype(jnp.bfloat16))[:, :1]
    return jnp.where(part > 0.0, best + before, -1.0)


def early_kernel(
    segments, where_ref, pads_ref, span_ref, widths_ref, gh_ref, gl_ref, wh_ref, wl_ref, rows_ref, needed_ref,
    square_ref, plane_ref,
):
    band = pl.program_id(0)
    where = where_ref[0]
    per = MAXW // BAND

    @pl.when(band == 0)
    def _():
        shift = iota((3 * REACH, REACH), 0) - REACH - iota((3 * REACH, REACH), 1)
        square_ref[...] = shift * shift
        plane_ref[...] = jnp.ones(plane_ref.shape, jnp.float32)
        plane_ref[0, 1 : segments + 1, :] = widths_ref[...].astype(jnp.float32)
        lanes = lax.broadcasted_iota(jnp.int32, (1, MAXW), 1)
        for segment in range(segments):
            line = jnp.full((1, MAXW), pads_ref[segment * per], jnp.int32)
            for k in range(1, per):
                line = jnp.where(lanes >= k * BAND, pads_ref[segment * per + k], line)
            plane_ref[1, segment + 1 : segment + 2, :] = line.astype(jnp.float32)
        rows_ref[...] = jnp.ones(rows_ref.shape, jnp.float32)
        for k in range(2):
            for j in range(4):
                rows_ref[4 * k + j : 4 * k + j + 1, :] = plane_ref[k, pl.ds(2 * where + j, 1), :]
            rows_ref[8 + k * segments : 8 + (k + 1) * segments, :] = plane_ref[k, 1 : segments + 1, :]
        columns = jnp.transpose(rows_ref[...])
        column = lambda k: columns[:, k : k + 1]
        index = iota((MAXW, 1), 0)
        lane = iota((1, MAXW), 1)

        for half, segment in ((0, 0), (1, 3)):
            width, pad = column(segment), column(4 + segment)
            depth = MAXW - 1.0 - index if half == 0 else index
            away = lane + 1.0 if half == 0 else MAXW - lane
            need, best, _ = cover(width, pad, depth)
            place = slots(need, best)
            chosen = jnp.where(place == lane, 1.0, 0.0).astype(jnp.bfloat16)
            high, low = split(wall_coeff(depth + away, rate_of(width), pad, inverse_norm(width, pad)))
            pick = lambda values: lax.dot_general(
                chosen, values, (((0,), (0,)), ((), ())), preferred_element_type=jnp.float32
            )
            plain = jnp.where((away == index + 1.0) & (index < best), 1.0, 0.0)
            wh_ref[half] = (pick(high) + plain).astype(jnp.bfloat16)
            wl_ref[half] = pick(low).astype(jnp.bfloat16)

        most = jnp.zeros((1, 1), jnp.float32)
        for segment in range(1, segments - 1):
            depth = MAXW - 1.0 - index if segment % 2 else index
            cost = cover(column(8 + segment), column(8 + segments + segment), depth)[2]
            most = jnp.maximum(most, cost)
        needed_ref[0, 0] = jnp.max(most).astype(jnp.int32)

    spread = jnp.full((1, 1), span_ref[where * pl.num_programs(0) + band], jnp.int32).astype(jnp.float32)
    rate = rate_of(spread)
    steps = iota((1, 4 * REACH), 1) - 2 * REACH
    profile = jnp.where(jnp.abs(steps) <= 2.0 * spread, jnp.exp(steps * steps * rate), 0.0)
    inverse = 1.0 / jnp.sqrt(jnp.sum(profile * profile, axis=1, keepdims=True))
    square = square_ref[...]
    coeffs = jnp.where(square <= 4.0 * spread * spread, jnp.exp(square * rate) * inverse, 0.0)
    gh_ref[0], gl_ref[0] = split(coeffs)


def early_tables(where, band_pads, span_widths, half_widths, bands):
    segments = half_widths.shape[0]
    toeplitz = jax.ShapeDtypeStruct((bands, 3 * REACH, REACH), jnp.bfloat16)
    give = jax.ShapeDtypeStruct((2, MAXW, MAXW), jnp.bfloat16)
    rows = jax.ShapeDtypeStruct((128, MAXW), jnp.float32)
    block = pl.BlockSpec((1, 3 * REACH, REACH), lambda b, *s: (b, 0, 0))
    whole = pl.BlockSpec((2, MAXW, MAXW), lambda b, *s: (0, 0, 0))
    gh, gl, wh, wl, rows, needed = pl.pallas_call(
        functools.partial(early_kernel, segments),
        grid_spec=pltpu.PrefetchScalarGridSpec(
            num_scalar_prefetch=3,
            grid=(bands,),
            in_specs=[pl.BlockSpec(half_widths.shape, lambda b, *s: (0, 0))],
            out_specs=[
                block, block, whole, whole,
                pl.BlockSpec(rows.shape, lambda b, *s: (0, 0)),
                pl.BlockSpec(memory_space=pltpu.SMEM),
            ],
            scratch_shapes=[
                pltpu.VMEM((3 * REACH, REACH), jnp.float32),
                pltpu.VMEM((2, segments + 8, MAXW), jnp.float32),
            ],
        ),
        out_shape=[toeplitz, toeplitz, give, give, rows, jax.ShapeDtypeStruct((1, 1), jnp.int32)],
        name="early",
    )(where, band_pads, span_widths, half_widths)
    return (gh, gl), (wh, wl), rows, needed[0, 0]


def late_kernel(where_ref, rows_ref, stress_ref, ah_ref, al_ref, hh_ref, hl_ref, lund_ref):
    half = pl.program_id(0)
    last = pl.num_programs(0) - 1
    stand = lambda k: jnp.transpose(jnp.broadcast_to(rows_ref[pl.ds(k, 1), :], (128, MAXW)))[:, :1]
    width, pad = stand(1 + half), stand(5 + half)
    index = iota((MAXW, 1), 0)
    lane = iota((1, MAXW), 1)
    rate, inverse = rate_of(width), inverse_norm(width, pad)
    depth = jnp.where(half == 0, index, MAXW - 1.0 - index)
    need, best, _ = cover(width, pad, depth)
    place = slots(need, best)
    plain = wall_coeff(depth + lane + 1.0, rate, pad, inverse)
    plain = jnp.where((place < 0.0) & (lane < best), plain, 0.0)
    take = jnp.where(place == lane, 1.0, plain)
    outer = jnp.where(half == 0, where_ref[0] == 0, where_ref[0] == where_ref[1] - 1)
    take = jnp.where(outer, 0.0, take)
    ah_ref[0], al_ref[0] = split(take)
    apart = jnp.abs(iota((1, 2 * MAXW), 1) - (index + (half * MAXW).astype(jnp.float32)))
    hh_ref[...], hl_ref[...] = split(wall_coeff(apart, rate, pad, inverse))

    @pl.when(half == last)
    def _():
        uu, vv, ww, uv, uw, vw = (stress_ref[k : k + 1, :] for k in range(6))
        lund_aa = jnp.sqrt(uu)
        lund_ba = uv / lund_aa
        lund_bb = jnp.sqrt(vv - lund_ba * lund_ba)
        lund_ca = uw / lund_aa
        lund_cb = (vw - lund_ba * lund_ca) / lund_bb
        lund_cc = jnp.sqrt(ww - lund_ca * lund_ca - lund_cb * lund_cb)
        mean = stress_ref[6:7, :]
        lines = [lund_aa, lund_ba, lund_bb, lund_ca, lund_cb, lund_cc, mean, mean]
        lines.append(jnp.zeros((120, stress_ref.shape[1]), jnp.float32))
        lund_ref[...] = jnp.transpose(jnp.concatenate(lines, axis=0))


def late_tables(where, rows, stress_rows):
    rows_here = stress_rows.shape[1]
    take = jax.ShapeDtypeStruct((2, MAXW, MAXW), jnp.bfloat16)
    local = jax.ShapeDtypeStruct((rows_here, rows_here), jnp.bfloat16)
    take_block = pl.BlockSpec((1, MAXW, MAXW), lambda h: (h, 0, 0))
    local_block = pl.BlockSpec((MAXW, rows_here), lambda h: (h, 0))
    ah, al, hh, hl, lund = pl.pallas_call(
        late_kernel,
        grid=(2,),
        in_specs=[pl.BlockSpec(memory_space=pltpu.SMEM), whole(rows), whole(stress_rows)],
        out_specs=[take_block, take_block, local_block, local_block, pl.BlockSpec((rows_here, 128), lambda h: (0, 0))],
        out_shape=[take, take, local, local, jax.ShapeDtypeStruct((rows_here, 128), jnp.float32)],
        name="late",
    )(where, rows, stress_rows)
    return (ah, al), (hh, hl), lund


def widened(block):
    zero = jnp.zeros((REACH, REACH), block.dtype)
    left = jnp.concatenate([block, zero], axis=0)
    return jnp.concatenate([left, jnp.concatenate([zero, block], axis=0)], axis=1)


def front_kernel(tile_range, pieces, x_ref, low_ref, high_ref, gh_ref, gl_ref, wh_ref, wl_ref, *rest):
    keep_high, keep_low = rest[-2:]
    sh_ref, sl_ref, *sends = rest[-4 - 2 * len(pieces) : -2]
    band = pl.program_id(0)
    per = MAXW // BAND
    first, last = tile_range
    wide = jnp.concatenate([low_ref[0], x_ref[0], high_ref[0]], axis=1)[:, first * TILE : (last + 1) * TILE]
    wide_high, wide_low = split(wide)
    count = last - first
    x_high = jnp.concatenate([wide_high[:, t * TILE : (t + 2) * TILE] for t in range(count)], axis=0)
    x_low = jnp.concatenate([wide_low[:, t * TILE : (t + 2) * TILE] for t in range(count)], axis=0)
    high, low = split(dot3(x_high, x_low, widened(gh_ref[0]), widened(gl_ref[0])))
    start = pl.multiple_of((band % per) * BAND, BAND)
    for t in range(count):
        cols = slice(t * TILE, (t + 1) * TILE)
        rows = slice(t * BAND, (t + 1) * BAND)
        sh_ref[0, :, cols] = high[rows]
        sl_ref[0, :, cols] = low[rows]
        keep_high[pl.ds(start, BAND), cols] = high[rows]
        keep_low[pl.ds(start, BAND), cols] = low[rows]

    for half in range(2):

        @pl.when(band == (per - 1 if half == 0 else pl.num_programs(0) - 1))
        def _(half=half):
            step = TILE
            for (left, right, top, end), send_ref in zip(pieces, sends[half::2]):

                def body(t, carry, left=left, top=top, end=end, send_ref=send_ref):
                    here = pl.ds(pl.multiple_of(t * step, step), step)
                    cols = pl.ds(pl.multiple_of(t * step + left, step), step)
                    send_ref[:, here] = dot3(
                        wh_ref[0, top:end, :], wl_ref[0, top:end, :], keep_high[:, cols], keep_low[:, cols]
                    )
                    return carry

                lax.fori_loop(0, (right - left) // step, body, 0)


def front(spans, field, low, high, tables, give, held, channel, cuts):
    channels, rows, cols = field.shape
    bands = rows // BAND
    tiles = cols // TILE
    width = cols // cuts
    size = spans[-1][1]
    pieces = [(k * width, (k + 1) * width, *span) for k in range(cuts) for span in spans]
    halo = pl.BlockSpec((1, BAND, REACH), lambda b: (max(channel - 1, 0), b, 0))
    toeplitz = pl.BlockSpec((1, 3 * REACH, REACH), lambda b: (b, 0, 0))
    half = pl.BlockSpec((1, size, MAXW), lambda b: (b * 2 // bands, 0, 0))
    line = pl.BlockSpec((1, BAND, cols), lambda b: (channel, b, 0))
    block = line
    in_specs = [line, halo, halo, toeplitz, toeplitz, half, half]
    operands = [field, low, high, *tables, *give]
    aliases = {}
    if held is not None:
        in_specs += [pl.BlockSpec(memory_space=pl.ANY)] * 2
        aliases = {len(operands): 0, len(operands) + 1: 1}
        operands += list(held)
    kept = jax.ShapeDtypeStruct((channels, rows, cols), jnp.bfloat16)
    sends = [jax.ShapeDtypeStruct((p[3] - p[2], width), jnp.float32) for p in pieces for _ in range(2)]
    results = pl.pallas_call(
        functools.partial(front_kernel, (0, tiles), pieces),
        grid=(bands,),
        in_specs=in_specs,
        out_specs=[block, block] + [whole(send) for send in sends],
        out_shape=[kept, kept] + sends,
        scratch_shapes=[pltpu.VMEM((MAXW, cols), jnp.bfloat16)] * 2,
        input_output_aliases=aliases,
        cost_estimate=pl.CostEstimate(
            flops=6 * rows * cols * 2 * TILE + 12 * size * MAXW * cols,
            bytes_accessed=rows * cols * 8 + size * cols * 8,
            transcendentals=0,
        ),
        name="front",
    )(*operands)
    return results[:2], [tuple(results[2 + 2 * k : 4 + 2 * k]) for k in range(len(pieces))]


def across(ah_ref, al_ref, half, recv):
    size = recv.shape[0]
    high, low = split(recv)
    return dot3(ah_ref[half, :, :size], al_ref[half, :, :size], high, low)


def main_kernel(counts, sh_ref, sl_ref, *rest):
    arrived = rest[: 2 * sum(counts)]
    ah_ref, al_ref, hh_ref, hl_ref, lund_ref, out_ref = rest[2 * sum(counts) :]

    def body(channel, carry):
        out_ref[channel] = dot3(hh_ref[...], hl_ref[...], sh_ref[channel], sl_ref[channel])
        return carry

    lax.fori_loop(0, sh_ref.shape[0], body, 0)

    def psi(channel):
        start = 2 * sum(counts[:channel])
        sums = []
        for half in range(2):
            parts = [ref[...] for ref in arrived[start + half : start + 2 * counts[channel] : 2]]
            sums.append(across(ah_ref, al_ref, half, jnp.concatenate(parts, axis=0)))
        return out_ref[channel] + jnp.concatenate(sums, axis=0)

    column = lambda k: lund_ref[:, k : k + 1]
    first, second = psi(0), psi(1)
    out_ref[0] = column(6) + column(0) * first
    out_ref[1] = column(1) * first + column(2) * second
    out_ref[2] = column(3) * first + column(4) * second + column(5) * out_ref[2]


ROOM = pltpu.CompilerParams(vmem_limit_bytes=56 * 1024 * 1024)


def main_filter(held, arrived, take, local, lund):
    channels, rows, cols = held[0].shape
    counts = tuple(len(pieces) for pieces in arrived)
    recv = [array for pieces in arrived for pair in pieces for array in pair]
    step = TILE
    block = pl.BlockSpec((channels, rows, step), lambda t: (0, 0, t))
    return pl.pallas_call(
        functools.partial(main_kernel, counts),
        grid=(cols // step,),
        in_specs=[block, block]
        + [pl.BlockSpec((array.shape[0], step), lambda t: (0, t)) for array in recv]
        + [whole(array) for array in (*take, *local, lund)],
        out_specs=block,
        out_shape=jax.ShapeDtypeStruct((channels, rows, cols), jnp.float32),
        compiler_params=ROOM,
        cost_estimate=pl.CostEstimate(
            flops=6 * channels * rows * rows * cols, bytes_accessed=channels * rows * cols * 8, transcendentals=0
        ),
        name="main",
    )(*held, *recv, *take, *local, lund)


def update_kernel(top, bottom, ah_ref, al_ref, lund_ref, out_in_ref, out_ref):
    def body(t, carry):
        cols = pl.ds(pl.multiple_of(t * TILE, TILE), TILE)
        for half, recv in ((0, top), (1, bottom)):
            rows = slice(half * MAXW, (half + 1) * MAXW)
            given = lund_ref[rows, 5:6] * across(ah_ref, al_ref, half, recv[:, cols])
            out_ref[0, rows, cols] = out_in_ref[0, rows, cols] + given
        return carry

    lax.fori_loop(0, out_ref.shape[2] // TILE, body, 0)


def update(out, arrived, take, lund, first):
    channels, rows, _ = out.shape
    size, width = arrived[0].shape
    step = 2 * TILE
    block = pl.BlockSpec((1, rows, step), lambda t: (channels - 1, 0, t + first // step))
    return pl.pallas_call(
        update_kernel,
        grid=(width // step,),
        in_specs=[pl.BlockSpec((size, step), lambda t: (0, t))] * 2
        + [whole(array) for array in (*take, lund)]
        + [block],
        out_specs=block,
        out_shape=jax.ShapeDtypeStruct(out.shape, out.dtype),
        input_output_aliases={5: 0},
        compiler_params=ROOM,
        cost_estimate=pl.CostEstimate(
            flops=6 * rows * size * width, bytes_accessed=rows * width * 8 + size * width * 8, transcendentals=0
        ),
        name="update",
    )(*arrived, *take, lund, out)


def ring(axis):
    count = lax.axis_size(axis)
    forward = [(i, (i + 1) % count) for i in range(count)]
    return forward, [(target, source) for source, target in forward]


def exchange(field):
    forward, backward = ring("span")
    low = lax.ppermute(field[:, :, -REACH:], "span", forward)
    return low, lax.ppermute(field[:, :, :REACH], "span", backward)


def shards(random_field, half_widths, band_pads, span_widths, stresses, mean_flow):
    _, rows_here, cols = random_field.shape
    wall_count = lax.axis_size("wall")
    where = jnp.stack([lax.axis_index("wall"), jnp.int32(wall_count)])
    halo = exchange(random_field[:1])
    tables, give, rows, needed = early_tables(
        where, band_pads, span_widths, half_widths.reshape(-1, MAXW), rows_here // BAND
    )
    rest, needed = lax.optimization_barrier((random_field, needed))
    halos = exchange(rest[1:])
    stress_rows = jnp.pad(jnp.concatenate([stresses, mean_flow[None]], axis=0), ((0, 1), (0, 0)))
    downward, upward = ring("wall")
    spans = list(zip((0,) + SIZES[:-1], SIZES))
    held, ahead = front(spans, random_field, *halo, tables, give, None, 0, 1)

    def across_edges(pieces):
        arrived = []
        for up, down in pieces:
            bottom = lax.ppermute(up, "wall", upward)
            arrived.append((lax.ppermute(down, "wall", downward), bottom))
        return arrived

    def run(number, *operands):
        return steps(number, *operands)

    def steps(number, field, halos, tables, give, where, rows, stress_rows, held, ahead):
        span = [(0, SIZES[number])]
        first = across_edges(ahead[: number + 1])
        held, pieces = front(span, field, *halos, tables, give, held, 1, 1)
        second = across_edges(pieces)
        held, pieces = front(span, field, *halos, tables, give, held, 2, 2)
        third = across_edges(pieces)
        take, local, lund = late_tables(where, rows, stress_rows)
        out = main_filter(held, (first, second), take, local, lund)
        for k, pair in enumerate(third):
            out = update(out, pair, take, lund, k * (cols // len(third)))
        return out

    operands = (random_field, halos, tables, give, where, rows, stress_rows, held, ahead)
    if len(SIZES) == 1:
        return run(0, *operands)
    which = sum((needed > size).astype(jnp.int32) for size in SIZES[:-1])
    return lax.switch(which, [functools.partial(run, k) for k in range(len(SIZES))], *operands)


def solution(mesh):
    return jax.shard_map(
        shards,
        mesh=mesh,
        in_specs=(P(None, "wall", "span"), P(), P(), P(), P(None, "wall"), P("wall")),
        out_specs=P(None, "wall", "span"),
        check_vma=False,
    )
```

profile of v0, /device:TPU:0, one launch (start us, length us, event | category | flops | bytes accessed | tf_op | source)
XLA Modules:
  0.0 180.8 jit_solution(6605727561330109524)
XLA Ops:
  0.0 1.8 fusion
  1.8 6.0 %collective-permute-start.33 = (f32[1,512,128]{2,1,0:T(8,128)}, f32[1,512,128]{2,1,0:T(8,128)}, u32[]{:S(2)}, u32[]{:S(2)}) collective-permute-start(f32[1,512,128]{2,1,0:T(8,128)} %get-tuple-element.231), channel_id=1, source_target_pairs={{4,0},{8,4},{12,8},{16,12},{20,16},{24,20},{28,24},{32,28},{36,32}... | collective-permute-start | bytes 786440 | tf_op jit(solution)/shard_map/ppermute | solution.py:396
  7.8 1.3 reshape.3.widths_ref
  9.2 5.4 %early.1 = (bf16[8,384,128]{2,1,0:T(8,128)(2,1)S(1)}, bf16[8,384,128]{2,1,0:T(8,128)(2,1)S(1)}, bf16[2,256,256]{2,1,0:T(8,128)(2,1)S(1)}, bf16[2,256,256]{2,1,0:...) custom-call(s32[2]{0:T(128)S(1)} %pad_add_fusion.where_ref, s32[32]{0:T(128)} %pads_ref.1, s32[32]{0:T(128)} %span_ref.1, ...), custom_call_target="tpu_custom_call" | custom-call | tf_op jit(solution)/shard_map/early/pallas_call | solution.py:139
  14.6 2.2 %fusion.1 = (f32[2,512,128]{2,1,0:T(8,128)}, f32[2,512,128]{2,1,0:T(8,128)}) fusion(f32[3,512,2048]{2,1,0:T(8,128)} %x_ref.1), kind=kLoop, calls=%fused_computation.4 | loop fusion | bytes 2097152 | tf_op jit(solution)/shard_map/slice | solution.py:396
  16.9 5.1 %collective-permute-start.31 = (f32[2,512,128]{2,1,0:T(8,128)}, f32[2,512,128]{2,1,0:T(8,128)S(1)}, u32[]{:S(2)}, u32[]{:S(2)}) collective-permute-start(f32[2,512,128]{2,1,0:T(8,128)} %get-tuple-element.233), channel_id=1, source_target_pairs={{4,0},{8,4},{12,8},{16,12},{20,16},{24,20},{28,24},{32,28},{36,32}... | collective-permute-start | bytes 1572872 | tf_op jit(solution)/shard_map/ppermute | solution.py:396
  24.0 20.6 %front.13 = (bf16[3,512,2048]{2,1,0:T(8,128)(2,1)}, bf16[3,512,2048]{2,1,0:T(8,128)(2,1)}, f32[152,2048]{1,0:T(8,128)}, f32[152,2048]{1,0:T(8,128)}, f32[32,2048...) custom-call(f32[3,512,2048]{2,1,0:T(8,128)} %x_ref.1, ...), custom_call_target="tpu_custom_call" | custom-call | flops 4831838208 | bytes 12582912 | tf_op jit(solution)/shard_map/front/pallas_call | solution.py:279
  44.6 136.2 %conditional.1 = (f32[3,512,2048]{2,1,0:T(8,128)}) conditional(s32[]{:T(128)} %clamp.3, (f32[3,512,2048]{2,1,0:T(8,128)}, f32[2,512,128]{2,1,0:T(8,128)S(1)}, f32[2,512,128]{2,1,0:T(8,128)S(1)}, bf16[8,384,128]{2,1,0:T(8,128)(2,1)S(1)}, bf16[8,384,128]{2,1,0:T(8,128)(2,1)S(1)}, /*index=5*/bf16[2,256,256]{2,1,0:T(8,128)(2,1)S(1)}, ...), branch_computations={%region_0.1_spmd, %region_1.2_spmd, %region_2.3_spmd} | conditional | flops 20937965568 | bytes 125829696 | solution.py:441
  44.8 13.7 %front.9 = (bf16[3,512,2048]{2,1,0:T(8,128)(2,1)}, bf16[3,512,2048]{2,1,0:T(8,128)(2,1)}, f32[184,2048]{1,0:T(8,128)}, f32[184,2048]{1,0:T(8,128)}) custom-call(f32[3,512,2048]{2,1,0:T(8,128)} %get-tuple-element.134.x_ref, f32[2,512,128]{2,1,0:T(8,128)S(1)} %get-tuple-element.135.low_ref, ...), custom_call_target="tpu_custom_call", output_to_operand_aliasing={{0}: (7, {}), {1}: (8, {})} | custom-call | flops 4378853376 | bytes 11403264 | tf_op jit(solution)/shard_map/cond/branch_1_fun/front/pallas_call | solution.py:279
  58.5 1.5 collective-permute-start.16
  60.0 1.8 collective-permute-start.17
  62.0 3.0 %collective-permute-start.13 = (f32[152,2048]{1,0:T(8,128)}, f32[152,2048]{1,0:T(8,128)}, u32[]{:S(2)}, u32[]{:S(2)}) collective-permute-start(f32[152,2048]{1,0:T(8,128)} %get-tuple-element.158), channel_id=1, source_target_pairs={{1,0},{2,1},{3,2},{0,3},{5,4},{6,5},{7,6},{4,7},{9,8},{10,9},{11,1... | collective-permute-start | bytes 3735560 | tf_op jit(solution)/shard_map/cond/branch_1_fun/ppermute | solution.py:417
  65.0 3.4 %late.4 = (bf16[2,256,256]{2,1,0:T(8,128)(2,1)}, bf16[2,256,256]{2,1,0:T(8,128)(2,1)}, bf16[512,512]{1,0:T(8,128)(2,1)}, bf16[512,512]{1,0:T(8,128)(2,1)}, f32[512,128]{1,0:T(8,128)}) custom-call(s32[2]{0:T(128)S(1)} %get-tuple-element.147.where_ref, f32[128,256]{1,0:T(8,128)S(1)} %get-tuple-element.148.rows_ref, f32[8,512]{1,0:T(8,128)S(1)} %get-tuple-element.149.stress_ref), custom_call_target="tpu_custom_call" | custom-call | tf_op jit(solution)/shard_map/cond/branch_1_fun/late/pallas_call | solution.py:202
  68.5 54.3 %collective-permute-done.14.rest_2_ = f32[32,2048]{1,0:T(8,128)} collective-permute-done((f32[32,2048]{1,0:T(8,128)}, f32[32,2048]{1,0:T(8,128)}, u32[]{:S(2)}, u32[]{:S(2)}) %collective-permute-start.14) | collective-permute-done | bytes 262176 | tf_op jit(solution)/shard_map/cond/branch_1_fun/ppermute | solution.py:418
  122.7 1.5 collective-permute-start.15
  124.3 13.7 %front.10 = (bf16[3,512,2048]{2,1,0:T(8,128)(2,1)}, bf16[3,512,2048]{2,1,0:T(8,128)(2,1)}, f32[184,1024]{1,0:T(8,128)}, f32[184,1024]{1,0:T(8,128)}, f32[184,1024]{1,0:T(8,128)}, /*index=5*/f32[184,1024]{1,0:T(8,128)}) custom-call(f32[3,512,2048]{2,1,0:T(8,128)} %get-tuple-element.134.x_ref, ...), custom_call_target="tpu_custom_call", output_to_operand_aliasing={{0}: (7, {}), {1}: (8, {})} | custom-call | flops 4378853376 | bytes 11403264 | tf_op jit(solution)/shard_map/cond/branch_1_fun/front/pallas_call | solution.py:279
  138.6 2.8 %collective-permute-start.9 = (f32[184,1024]{1,0:T(8,128)}, f32[184,1024]{1,0:T(8,128)S(1)}, u32[]{:S(2)}, u32[]{:S(2)}) collective-permute-start(f32[184,1024]{1,0:T(8,128)} %get-tuple-element.146), channel_id=1, source_target_pairs={{1,0},{2,1},{3,2},{0,3},{5,4},{6,5},{7,6},{4,7},{9,8},{10,9},{11,1... | collective-permute-start | bytes 2261000 | tf_op jit(solution)/shard_map/cond/branch_1_fun/ppermute | solution.py:417
  141.3 3.2 %collective-permute-start.11 = (f32[184,1024]{1,0:T(8,128)}, f32[184,1024]{1,0:T(8,128)S(1)}, u32[]{:S(2)}, u32[]{:S(2)}) collective-permute-start(f32[184,1024]{1,0:T(8,128)} %get-tuple-element.154), channel_id=1, source_target_pairs={{1,0},{2,1},{3,2},{0,3},{5,4},{6,5},{7,6},{4,7},{9,8},{10,9},{11,1... | collective-permute-start | bytes 2261000 | tf_op jit(solution)/shard_map/cond/branch_1_fun/ppermute | solution.py:417
  144.6 23.8 %main.4.out_in_ref = f32[3,512,2048]{2,1,0:T(8,128)} custom-call(bf16[3,512,2048]{2,1,0:T(8,128)(2,1)} %get-tuple-element.155.sh_ref, bf16[3,512,2048]{2,1,0:T(8,128)(2,1)} %get-tuple-element.156.sl_ref, f32[152,2048]{1,0:T(8,128)} %collective-permute-done.12.rest_0_, f32[152,2048]{1,0:T(8,128)} %collective-permute-done.13.rest_1_, ...), custom_call_target="tpu_custom_call" | custom-call | flops 9663676416 | bytes 25165824 | tf_op jit(solution)/shard_map/cond/branch_1_fun/main/pallas_call | solution.py:337
  168.7 0.9 copy-done.5
  169.6 0.9 copy-done.6
  170.5 4.3 %update.8.out_in_ref = f32[3,512,2048]{2,1,0:T(8,128)} custom-call(f32[184,1024]{1,0:T(8,128)} %copy-done.5, f32[184,1024]{1,0:T(8,128)} %copy-done.6, bf16[2,256,256]{2,1,0:T(8,128)(2,1)} %get-tuple-element.150.rest_6_.ah_ref, bf16[2,256,256]{2,1,0:T(8,128)(2,1)} %get-tuple-element.151.rest_7_.al_ref, ...), custom_call_target="tpu_custom_call", output_to_operand_aliasing={{}: (5, {})} | custom-call | flops 578813952 | bytes 5701632 | tf_op jit(solution)/shard_map/cond/branch_1_fun/update/pallas_call | solution.py:370
  175.6 0.9 copy-done.4
  176.5 4.3 %update.9 = f32[3,512,2048]{2,1,0:T(8,128)} custom-call(f32[184,1024]{1,0:T(8,128)} %copy-done.3, f32[184,1024]{1,0:T(8,128)} %copy-done.4, bf16[2,256,256]{2,1,0:T(8,128)(2,1)} %get-tuple-element.150.rest_6_.ah_ref, bf16[2,256,256]{2,1,0:T(8,128)(2,1)} %get-tuple-element.151.rest_7_.al_ref, ...), custom_call_target="tpu_custom_call", output_to_operand_aliasing={{}: (5, {})} | custom-call | flops 578813952 | bytes 5701632 | tf_op jit(solution)/shard_map/cond/branch_1_fun/update/pallas_call | solution.py:370
  (32 shorter events, 2.9 us)
Async XLA Ops:
  1.8 22.2 %collective-permute-start.33 = (f32[1,512,128]{2,1,0:T(8,128)}, f32[1,512,128]{2,1,0:T(8,128)}, u32[]{:S(2)}, u32[]{:S(2)}) collective-permute-start(f32[1,512,128]{2,1,0:T(8,128)} %get-tuple-element.231), channel_id=1, source_target_pairs={{4,0},{8,4},{12,8},{16,12},{20,16},{24,20},{28,24},{32,28},{36,32}... | collective-permute-start | bytes 786440 | tf_op jit(solution)/shard_map/ppermute | solution.py:396
  7.8 16.1 %collective-permute-start.32 = (f32[1,512,128]{2,1,0:T(8,128)S(1)}, f32[1,512,128]{2,1,0:T(8,128)}, u32[]{:S(2)}, u32[]{:S(2)}) collective-permute-start(f32[1,512,128]{2,1,0:T(8,128)S(1)} %get-tuple-element.232), channel_id=1, source_target_pairs={{0,4},{4,8},{8,12},{12,16},{16,20},{20,24},{24,28},{28,32},{32,36}... | collective-permute-start | bytes 786440 | tf_op jit(solution)/shard_map/ppermute | solution.py:395
  9.2 14.0 %copy-start.11 = (s32[2]{0:T(128)}, s32[2]{0:T(128)S(1)}, u32[]{:S(2)}) copy-start(s32[2]{0:T(128)S(1)} %pad_add_fusion.where_ref) | copy-start | bytes 28
  16.9 27.7 %collective-permute-start.31 = (f32[2,512,128]{2,1,0:T(8,128)}, f32[2,512,128]{2,1,0:T(8,128)S(1)}, u32[]{:S(2)}, u32[]{:S(2)}) collective-permute-start(f32[2,512,128]{2,1,0:T(8,128)} %get-tuple-element.233), channel_id=1, source_target_pairs={{4,0},{8,4},{12,8},{16,12},{20,16},{24,20},{28,24},{32,28},{36,32}... | collective-permute-start | bytes 1572872 | tf_op jit(solution)/shard_map/ppermute | solution.py:396
  21.9 22.7 %collective-permute-start.30 = (f32[2,512,128]{2,1,0:T(8,128)}, f32[2,512,128]{2,1,0:T(8,128)S(1)}, u32[]{:S(2)}, u32[]{:S(2)}) collective-permute-start(f32[2,512,128]{2,1,0:T(8,128)} %get-tuple-element.234), channel_id=1, source_target_pairs={{0,4},{4,8},{8,12},{12,16},{16,20},{20,24},{24,28},{28,32},{32,36}... | collective-permute-start | bytes 1572872 | tf_op jit(solution)/shard_map/ppermute | solution.py:395
  24.0 20.6 %copy-start.12 = (s32[2]{0:T(128)S(1)}, s32[2]{0:T(128)}, u32[]{:S(2)}) copy-start(s32[2]{0:T(128)} %copy-done.11) | copy-start | bytes 28
  58.5 82.8 %collective-permute-start.16 = (f32[184,2048]{1,0:T(8,128)}, f32[184,2048]{1,0:T(8,128)}, u32[]{:S(2)}, u32[]{:S(2)}) collective-permute-start(f32[184,2048]{1,0:T(8,128)} %get-tuple-element.161), channel_id=1, source_target_pairs={{0,1},{1,2},{2,3},{3,0},{4,5},{5,6},{6,7},{7,4},{8,9},{9,10},{10,1... | collective-permute-start | bytes 4521992 | tf_op jit(solution)/shard_map/cond/branch_1_fun/ppermute | solution.py:418
  60.0 84.6 %collective-permute-start.17 = (f32[184,2048]{1,0:T(8,128)}, f32[184,2048]{1,0:T(8,128)}, u32[]{:S(2)}, u32[]{:S(2)}) collective-permute-start(f32[184,2048]{1,0:T(8,128)} %get-tuple-element.162), channel_id=1, source_target_pairs={{1,0},{2,1},{3,2},{0,3},{5,4},{6,5},{7,6},{4,7},{9,8},{10,9},{11,1... | collective-permute-start | bytes 4521992 | tf_op jit(solution)/shard_map/cond/branch_1_fun/ppermute | solution.py:417
  61.8 76.8 %collective-permute-start.12 = (f32[152,2048]{1,0:T(8,128)}, f32[152,2048]{1,0:T(8,128)}, u32[]{:S(2)}, u32[]{:S(2)}) collective-permute-start(f32[152,2048]{1,0:T(8,128)} %get-tuple-element.157), channel_id=1, source_target_pairs={{0,1},{1,2},{2,3},{3,0},{4,5},{5,6},{6,7},{7,4},{8,9},{9,10},{10,1... | collective-permute-start | bytes 3735560 | tf_op jit(solution)/shard_map/cond/branch_1_fun/ppermute | solution.py:418
  62.0 79.3 %collective-permute-start.13 = (f32[152,2048]{1,0:T(8,128)}, f32[152,2048]{1,0:T(8,128)}, u32[]{:S(2)}, u32[]{:S(2)}) collective-permute-start(f32[152,2048]{1,0:T(8,128)} %get-tuple-element.158), channel_id=1, source_target_pairs={{1,0},{2,1},{3,2},{0,3},{5,4},{6,5},{7,6},{4,7},{9,8},{10,9},{11,1... | collective-permute-start | bytes 3735560 | tf_op jit(solution)/shard_map/cond/branch_1_fun/ppermute | solution.py:417
  65.0 57.7 %collective-permute-start.14 = (f32[32,2048]{1,0:T(8,128)}, f32[32,2048]{1,0:T(8,128)}, u32[]{:S(2)}, u32[]{:S(2)}) collective-permute-start(f32[32,2048]{1,0:T(8,128)} %get-tuple-element.159), channel_id=1, source_target_pairs={{0,1},{1,2},{2,3},{3,0},{4,5},{5,6},{6,7},{7,4},{8,9},{9,10},{10,1... | collective-permute-start | bytes 786440 | tf_op jit(solution)/shard_map/cond/branch_1_fun/ppermute | solution.py:418
  122.7 15.3 %collective-permute-start.15 = (f32[32,2048]{1,0:T(8,128)}, f32[32,2048]{1,0:T(8,128)S(1)}, u32[]{:S(2)}, u32[]{:S(2)}) collective-permute-start(f32[32,2048]{1,0:T(8,128)} %get-tuple-element.160), channel_id=1, source_target_pairs={{1,0},{2,1},{3,2},{0,3},{5,4},{6,5},{7,6},{4,7},{9,8},{10,9},{11,1... | collective-permute-start | bytes 786440 | tf_op jit(solution)/shard_map/cond/branch_1_fun/ppermute | solution.py:417
  138.0 6.6 %copy-start.13 = (f32[32,2048]{1,0:T(8,128)}, f32[32,2048]{1,0:T(8,128)S(1)}, u32[]{:S(2)}) copy-start(f32[32,2048]{1,0:T(8,128)S(1)} %collective-permute-done.15.rest_3_) | copy-start | bytes 786436 | tf_op jit(solution)/shard_map/cond
  138.0 36.7 %collective-permute-start.8 = (f32[184,1024]{1,0:T(8,128)}, f32[184,1024]{1,0:T(8,128)S(1)}, u32[]{:S(2)}, u32[]{:S(2)}) collective-permute-start(f32[184,1024]{1,0:T(8,128)} %get-tuple-element.145), channel_id=1, source_target_pairs={{0,1},{1,2},{2,3},{3,0},{4,5},{5,6},{6,7},{7,4},{8,9},{9,10},{10,1... | collective-permute-start | bytes 2261000 | tf_op jit(solution)/shard_map/cond/branch_1_fun/ppermute | solution.py:418
  138.6 36.2 %collective-permute-start.9 = (f32[184,1024]{1,0:T(8,128)}, f32[184,1024]{1,0:T(8,128)S(1)}, u32[]{:S(2)}, u32[]{:S(2)}) collective-permute-start(f32[184,1024]{1,0:T(8,128)} %get-tuple-element.146), channel_id=1, source_target_pairs={{1,0},{2,1},{3,2},{0,3},{5,4},{6,5},{7,6},{4,7},{9,8},{10,9},{11,1... | collective-permute-start | bytes 2261000 | tf_op jit(solution)/shard_map/cond/branch_1_fun/ppermute | solution.py:417
  141.3 27.4 %collective-permute-start.10 = (f32[184,1024]{1,0:T(8,128)}, f32[184,1024]{1,0:T(8,128)S(1)}, u32[]{:S(2)}, u32[]{:S(2)}) collective-permute-start(f32[184,1024]{1,0:T(8,128)} %get-tuple-element.153), channel_id=1, source_target_pairs={{0,1},{1,2},{2,3},{3,0},{4,5},{5,6},{6,7},{7,4},{8,9},{9,10},{10,1... | collective-permute-start | bytes 2261000 | tf_op jit(solution)/shard_map/cond/branch_1_fun/ppermute | solution.py:418
  141.3 27.4 %collective-permute-start.11 = (f32[184,1024]{1,0:T(8,128)}, f32[184,1024]{1,0:T(8,128)S(1)}, u32[]{:S(2)}, u32[]{:S(2)}) collective-permute-start(f32[184,1024]{1,0:T(8,128)} %get-tuple-element.154), channel_id=1, source_target_pairs={{1,0},{2,1},{3,2},{0,3},{5,4},{6,5},{7,6},{4,7},{9,8},{10,9},{11,1... | collective-permute-start | bytes 2261000 | tf_op jit(solution)/shard_map/cond/branch_1_fun/ppermute | solution.py:417
  168.7 0.9 copy-start.5
  169.6 0.9 copy-start.6
  174.8 0.9 copy-start.3
  175.6 0.9 copy-start.4
where the time goes:
time: 183 us; the launch traced here: 181 us
  Pallas kernels  89.2 us (49%)
  waiting for transfers between devices  54.7 us (30%)
  starting transfers between devices  25.7 us (14%)
  local copies, waits for them, and re-layouts  8.81 us (5%)
    ppermute x5, waiting for transfers between devices, across_edges(): arrived.append((lax.ppermute(down, 'wall', downward), bottom))  54.6 us
    pallas_call x3, Pallas kernels, front(): pl.pallas_call(functools.partial(front_kernel, (0, tiles), pieces), grid=...  48 us
    pallas_call x1, Pallas kernels, main_filter(): pl.pallas_call(functools.partial(main_kernel, counts), grid=(cols // step...  23.8 us
    ppermute x5, starting transfers between devices, across_edges(): bottom = lax.ppermute(up, 'wall', upward)  12.3 us
    ppermute x2, starting transfers between devices, exchange(): return (low, lax.ppermute(field[:, :, :REACH], 'span', backward))  11.1 us
    pallas_call x2, Pallas kernels, update(): pl.pallas_call(update_kernel, grid=(width // step,), in_specs=[pl.BlockSp...  8.56 us
    pallas_call x1, Pallas kernels, early_tables(): pl.pallas_call(functools.partial(early_kernel, segments), grid_spec=pltpu...  5.43 us
    slice x2, local copies, waits for them, and re-layouts, exchange(): return (low, lax.ppermute(field[:, :, :REACH], 'span', backward))  4.01 us
  transfers between devices with their start and end apart: 14, of which 2 were waited for; matrix products, arithmetic and copies ran while one was open for 2% of the time, Pallas kernels for 39%

commit v1 on v0

v1 whole, which is shorter than its diff:
```python
import functools

import jax
import jax.numpy as jnp
from jax import lax
from jax.experimental import pallas as pl
from jax.experimental.pallas import tpu as pltpu
from jax.sharding import PartitionSpec as P

MAXW = 256
SPMAX = 64
BAND = 64
REACH = 2 * SPMAX
TILE = 4 * SPMAX
SIZES = (152, 184, 256)


def split(values):
    high = values.astype(jnp.bfloat16)
    return high, (values - high.astype(jnp.float32)).astype(jnp.bfloat16)


def dot(left, right):
    return lax.dot_general(left, right, (((1,), (0,)), ((), ())), preferred_element_type=jnp.float32)


def dot3(left_high, left_low, right_high, right_low):
    return dot(left_high, right_high) + (dot(left_high, right_low) + dot(left_low, right_high))


def whole(array):
    return pl.BlockSpec(array.shape, lambda *_: (0,) * len(array.shape))


def iota(shape, axis):
    return lax.broadcasted_iota(jnp.int32, shape, axis).astype(jnp.float32)


def wall_coeff(distance, rate, pad, inverse):
    return jnp.where(distance <= pad, jnp.exp(distance * distance * rate) * inverse, 0.0)


def rate_of(width):
    return (-0.5 * jnp.pi) / (width * width)


def inverse_norm(width, pad):
    steps = iota((1, MAXW + 128), 1)
    profile = wall_coeff(steps, rate_of(width), pad, 1.0)
    return 1.0 / jnp.sqrt(2.0 * jnp.sum(profile * profile, axis=1, keepdims=True) - 1.0)


def cover(width, pad, depth):
    need = jnp.floor(jnp.minimum(pad, width * 8.25)) - depth
    counts = iota((1, MAXW + 128), 1)
    total = jnp.sum(jnp.where(need > counts, 1.0, 0.0), axis=0, keepdims=True) + counts
    key = jnp.min(jnp.where(counts <= MAXW, total, 4096.0) * 512.0 + counts, axis=1, keepdims=True)
    cost = jnp.floor(key * (1.0 / 512.0))
    best = key - cost * 512.0
    return need, best, cost


def slots(need, best):
    part = jnp.where(need > best, 1.0, 0.0)
    earlier = jnp.where(iota((MAXW, MAXW), 1) < iota((MAXW, MAXW), 0), 1.0, 0.0).astype(jnp.bfloat16)
    before = dot(earlier, jnp.broadcast_to(part, (MAXW, 128)).astype(jnp.bfloat16))[:, :1]
    return jnp.where(part > 0.0, best + before, -1.0)


def early_kernel(
    segments, where_ref, pads_ref, widths_ref, wh_ref, wl_ref, rows_ref, needed_ref, plane_ref
):
    where = where_ref[0]
    per = MAXW // BAND

    plane_ref[...] = jnp.ones(plane_ref.shape, jnp.float32)
    widths = widths_ref[...].astype(jnp.float32)
    split_by = MAXW // widths.shape[1]
    lanes = lax.broadcasted_iota(jnp.int32, (1, MAXW), 1)
    for segment in range(segments):
        parts = [widths[segment * split_by + k : segment * split_by + k + 1] for k in range(split_by)]
        plane_ref[0, segment + 1 : segment + 2, :] = jnp.concatenate(parts, axis=1)
        line = jnp.full((1, MAXW), pads_ref[segment * per], jnp.int32)
        for k in range(1, per):
            line = jnp.where(lanes >= k * BAND, pads_ref[segment * per + k], line)
        plane_ref[1, segment + 1 : segment + 2, :] = line.astype(jnp.float32)
    rows_ref[...] = jnp.ones(rows_ref.shape, jnp.float32)
    for k in range(2):
        for j in range(4):
            rows_ref[4 * k + j : 4 * k + j + 1, :] = plane_ref[k, pl.ds(2 * where + j, 1), :]
        rows_ref[8 + k * segments : 8 + (k + 1) * segments, :] = plane_ref[k, 1 : segments + 1, :]
    columns = jnp.transpose(rows_ref[...])
    column = lambda k: columns[:, k : k + 1]
    index = iota((MAXW, 1), 0)
    lane = iota((1, MAXW), 1)

    for half, segment in ((0, 0), (1, 3)):
        width, pad = column(segment), column(4 + segment)
        depth = MAXW - 1.0 - index if half == 0 else index
        away = lane + 1.0 if half == 0 else MAXW - lane
        need, best, _ = cover(width, pad, depth)
        place = slots(need, best)
        chosen = jnp.where(place == lane, 1.0, 0.0).astype(jnp.bfloat16)
        high, low = split(wall_coeff(depth + away, rate_of(width), pad, inverse_norm(width, pad)))
        pick = lambda values: lax.dot_general(
            chosen, values, (((0,), (0,)), ((), ())), preferred_element_type=jnp.float32
        )
        plain = jnp.where((away == index + 1.0) & (index < best), 1.0, 0.0)
        wh_ref[half] = (pick(high) + plain).astype(jnp.bfloat16)
        wl_ref[half] = pick(low).astype(jnp.bfloat16)

    most = jnp.zeros((1, 1), jnp.float32)
    for segment in range(1, segments - 1):
        depth = MAXW - 1.0 - index if segment % 2 else index
        cost = cover(column(8 + segment), column(8 + segments + segment), depth)[2]
        most = jnp.maximum(most, cost)
    needed_ref[0, 0] = jnp.max(most).astype(jnp.int32)


def early_tables(where, band_pads, half_widths):
    segments = half_widths.shape[0] // MAXW
    half_widths = half_widths.reshape(-1, 128)
    give = jax.ShapeDtypeStruct((2, MAXW, MAXW), jnp.bfloat16)
    rows = jax.ShapeDtypeStruct((128, MAXW), jnp.float32)
    smem = pl.BlockSpec(memory_space=pltpu.SMEM)
    vmem = pl.BlockSpec(memory_space=pltpu.VMEM)
    wh, wl, rows, needed = pl.pallas_call(
        functools.partial(early_kernel, segments),
        in_specs=[smem, smem, vmem],
        out_specs=[vmem, vmem, vmem, smem],
        out_shape=[give, give, rows, jax.ShapeDtypeStruct((1, 1), jnp.int32)],
        scratch_shapes=[pltpu.VMEM((2, segments + 8, MAXW), jnp.float32)],
        name="early",
    )(where, band_pads, half_widths)
    return (wh, wl), rows, needed[0, 0]


def late_kernel(where_ref, rows_ref, stress_ref, ah_ref, al_ref, hh_ref, hl_ref, lund_ref):
    half = pl.program_id(0)
    last = pl.num_programs(0) - 1
    stand = lambda k: jnp.transpose(jnp.broadcast_to(rows_ref[pl.ds(k, 1), :], (128, MAXW)))[:, :1]
    width, pad = stand(1 + half), stand(5 + half)
    index = iota((MAXW, 1), 0)
    lane = iota((1, MAXW), 1)
    rate, inverse = rate_of(width), inverse_norm(width, pad)
    depth = jnp.where(half == 0, index, MAXW - 1.0 - index)
    need, best, _ = cover(width, pad, depth)
    place = slots(need, best)
    plain = wall_coeff(depth + lane + 1.0, rate, pad, inverse)
    plain = jnp.where((place < 0.0) & (lane < best), plain, 0.0)
    take = jnp.where(place == lane, 1.0, plain)
    outer = jnp.where(half == 0, where_ref[0] == 0, where_ref[0] == where_ref[1] - 1)
    take = jnp.where(outer, 0.0, take)
    ah_ref[0], al_ref[0] = split(take)
    apart = jnp.abs(iota((1, 2 * MAXW), 1) - (index + (half * MAXW).astype(jnp.float32)))
    hh_ref[...], hl_ref[...] = split(wall_coeff(apart, rate, pad, inverse))

    @pl.when(half == last)
    def _():
        uu, vv, ww, uv, uw, vw = (stress_ref[k : k + 1, :] for k in range(6))
        lund_aa = jnp.sqrt(uu)
        lund_ba = uv / lund_aa
        lund_bb = jnp.sqrt(vv - lund_ba * lund_ba)
        lund_ca = uw / lund_aa
        lund_cb = (vw - lund_ba * lund_ca) / lund_bb
        lund_cc = jnp.sqrt(ww - lund_ca * lund_ca - lund_cb * lund_cb)
        mean = stress_ref[6:7, :]
        lines = [lund_aa, lund_ba, lund_bb, lund_ca, lund_cb, lund_cc, mean, mean]
        lines.append(jnp.zeros((120, stress_ref.shape[1]), jnp.float32))
        lund_ref[...] = jnp.transpose(jnp.concatenate(lines, axis=0))


def late_tables(where, rows, stress_rows):
    rows_here = stress_rows.shape[1]
    take = jax.ShapeDtypeStruct((2, MAXW, MAXW), jnp.bfloat16)
    local = jax.ShapeDtypeStruct((rows_here, rows_here), jnp.bfloat16)
    take_block = pl.BlockSpec((1, MAXW, MAXW), lambda h: (h, 0, 0))
    local_block = pl.BlockSpec((MAXW, rows_here), lambda h: (h, 0))
    ah, al, hh, hl, lund = pl.pallas_call(
        late_kernel,
        grid=(2,),
        in_specs=[pl.BlockSpec(memory_space=pltpu.SMEM), whole(rows), whole(stress_rows)],
        out_specs=[take_block, take_block, local_block, local_block, pl.BlockSpec((rows_here, 128), lambda h: (0, 0))],
        out_shape=[take, take, local, local, jax.ShapeDtypeStruct((rows_here, 128), jnp.float32)],
        name="late",
    )(where, rows, stress_rows)
    return (ah, al), (hh, hl), lund


def widened(block):
    zero = jnp.zeros((REACH, REACH), block.dtype)
    left = jnp.concatenate([block, zero], axis=0)
    return jnp.concatenate([left, jnp.concatenate([zero, block], axis=0)], axis=1)


def span_block(square_ref, span):
    spread = jnp.full((1, 1), span, jnp.int32).astype(jnp.float32)
    rate = rate_of(spread)
    steps = iota((1, 4 * REACH), 1) - 2 * REACH
    profile = jnp.where(jnp.abs(steps) <= 2.0 * spread, jnp.exp(steps * steps * rate), 0.0)
    inverse = 1.0 / jnp.sqrt(jnp.sum(profile * profile, axis=1, keepdims=True))
    square = square_ref[...]
    return split(jnp.where(square <= 4.0 * spread * spread, jnp.exp(square * rate) * inverse, 0.0))


def front_kernel(build, cuts, spans, *refs):
    band = pl.program_id(0)
    if build:
        where_ref, span_ref, *refs = refs
        *refs, square_ref = refs
    x_ref, low_ref, high_ref, wh_ref, wl_ref, gh_ref, gl_ref = refs[:7]
    if build:
        refs = refs[7:]

        @pl.when(band == 0)
        def _():
            shift = iota((3 * REACH, REACH), 0) - REACH - iota((3 * REACH, REACH), 1)
            square_ref[...] = shift * shift

        block_high, block_low = span_block(square_ref, span_ref[where_ref[0] * pl.num_programs(0) + band])
        gh_ref[0], gl_ref[0] = block_high, block_low
    else:
        refs = refs[9:]
        block_high, block_low = gh_ref[0], gl_ref[0]
    sh_ref, sl_ref, *sends, keep_high, keep_low = refs
    per = MAXW // BAND
    tiles = x_ref.shape[2] // TILE
    wide = jnp.concatenate([low_ref[0], x_ref[0], high_ref[0]], axis=1)
    wide_high, wide_low = split(wide)
    x_high = jnp.concatenate([wide_high[:, t * TILE : (t + 2) * TILE] for t in range(tiles)], axis=0)
    x_low = jnp.concatenate([wide_low[:, t * TILE : (t + 2) * TILE] for t in range(tiles)], axis=0)
    high, low = split(dot3(x_high, x_low, widened(block_high), widened(block_low)))
    start = pl.multiple_of((band % per) * BAND, BAND)
    for t in range(tiles):
        cols = slice(t * TILE, (t + 1) * TILE)
        rows = slice(t * BAND, (t + 1) * BAND)
        sh_ref[0, :, cols] = high[rows]
        sl_ref[0, :, cols] = low[rows]
        keep_high[pl.ds(start, BAND), cols] = high[rows]
        keep_low[pl.ds(start, BAND), cols] = low[rows]

    for half in range(2):

        @pl.when(band == (per - 1 if half == 0 else pl.num_programs(0) - 1))
        def _(half=half):
            step = 2 * TILE
            width = x_ref.shape[2] // cuts
            for cut in range(cuts):
                refs_here = sends[2 * cut * len(spans) + half : 2 * (cut + 1) * len(spans) : 2]

                def body(t, carry, cut=cut, refs_here=refs_here):
                    here = pl.ds(pl.multiple_of(t * step, step), step)
                    cols = pl.ds(pl.multiple_of(t * step + cut * width, step), step)
                    value = dot3(wh_ref[0], wl_ref[0], keep_high[:, cols], keep_low[:, cols])
                    for (top, end), send_ref in zip(spans, refs_here):
                        send_ref[:, here] = value[top:end]
                    return carry

                lax.fori_loop(0, width // step, body, 0)


def front(spans, field, low, high, tables, give, held, channel, cuts, where=None, span_widths=None):
    channels, rows, cols = field.shape
    build = tables is None
    bands = rows // BAND
    width = cols // cuts
    size = spans[-1][1]
    pieces = [span for _ in range(cuts) for span in spans]
    halo = pl.BlockSpec((1, BAND, REACH), lambda b: (max(channel - 1, 0), b, 0))
    toeplitz = pl.BlockSpec((1, 3 * REACH, REACH), lambda b: (b, 0, 0))
    half = pl.BlockSpec((1, size, MAXW), lambda b: (b * 2 // bands, 0, 0))
    line = pl.BlockSpec((1, BAND, cols), lambda b: (channel, b, 0))
    in_specs = [line, halo, halo, half, half]
    operands = [field, low, high, *give]
    kept = jax.ShapeDtypeStruct((channels, rows, cols), jnp.bfloat16)
    sends = [jax.ShapeDtypeStruct((end - top, width), jnp.float32) for top, end in pieces for _ in range(2)]
    out_specs = [line, line] + [whole(send) for send in sends]
    out_shape = [kept, kept] + sends
    scratch = [pltpu.VMEM((MAXW, cols), jnp.bfloat16)] * 2
    aliases = {}
    if build:
        in_specs = [pl.BlockSpec(memory_space=pltpu.SMEM)] * 2 + in_specs
        operands = [where, span_widths] + operands
        out_specs = [toeplitz, toeplitz] + out_specs
        out_shape = [jax.ShapeDtypeStruct((bands, 3 * REACH, REACH), jnp.bfloat16)] * 2 + out_shape
        scratch = scratch + [pltpu.VMEM((3 * REACH, REACH), jnp.float32)]
    else:
        in_specs = in_specs + [toeplitz, toeplitz] + [pl.BlockSpec(memory_space=pl.ANY)] * 2
        operands = operands + [*tables, *held]
        aliases = {len(operands) - 2: 0, len(operands) - 1: 1}
    results = pl.pallas_call(
        functools.partial(front_kernel, build, cuts, spans),
        grid=(bands,),
        in_specs=in_specs,
        out_specs=out_specs,
        out_shape=out_shape,
        scratch_shapes=scratch,
        input_output_aliases=aliases,
        cost_estimate=pl.CostEstimate(
            flops=6 * rows * cols * 2 * TILE + 12 * size * MAXW * cols,
            bytes_accessed=rows * cols * 8 + size * cols * 8,
            transcendentals=0,
        ),
        name="front",
    )(*operands)
    if build:
        tables, results = results[:2], results[2:]
    outs = results[:2], [tuple(results[2 + 2 * k : 4 + 2 * k]) for k in range(len(pieces))]
    return (tables, *outs) if build else outs


def across(ah_ref, al_ref, half, recv):
    size = recv.shape[0]
    high, low = split(recv)
    return dot3(ah_ref[half, :, :size], al_ref[half, :, :size], high, low)


def main_kernel(counts, sh_ref, sl_ref, *rest):
    arrived = rest[: 2 * sum(counts)]
    ah_ref, al_ref, hh_ref, hl_ref, lund_ref, out_ref = rest[2 * sum(counts) :]

    def body(channel, carry):
        out_ref[channel] = dot3(hh_ref[...], hl_ref[...], sh_ref[channel], sl_ref[channel])
        return carry

    lax.fori_loop(0, sh_ref.shape[0], body, 0)

    def psi(channel):
        start = 2 * sum(counts[:channel])
        sums = []
        for half in range(2):
            parts = [ref[...] for ref in arrived[start + half : start + 2 * counts[channel] : 2]]
            sums.append(across(ah_ref, al_ref, half, jnp.concatenate(parts, axis=0)))
        return out_ref[channel] + jnp.concatenate(sums, axis=0)

    column = lambda k: lund_ref[:, k : k + 1]
    first, second = psi(0), out_ref[1]
    out_ref[0] = column(6) + column(0) * first
    out_ref[1] = column(1) * first + column(2) * second
    out_ref[2] = column(3) * first + column(4) * second + column(5) * out_ref[2]


ROOM = pltpu.CompilerParams(vmem_limit_bytes=56 * 1024 * 1024)


def main_filter(held, arrived, take, local, lund):
    channels, rows, cols = held[0].shape
    counts = tuple(len(pieces) for pieces in arrived)
    recv = [array for pieces in arrived for pair in pieces for array in pair]
    step = TILE
    block = pl.BlockSpec((channels, rows, step), lambda t: (0, 0, t))
    return pl.pallas_call(
        functools.partial(main_kernel, counts),
        grid=(cols // step,),
        in_specs=[block, block]
        + [pl.BlockSpec((array.shape[0], step), lambda t: (0, t)) for array in recv]
        + [whole(array) for array in (*take, *local, lund)],
        out_specs=block,
        out_shape=jax.ShapeDtypeStruct((channels, rows, cols), jnp.float32),
        compiler_params=ROOM,
        cost_estimate=pl.CostEstimate(
            flops=6 * channels * rows * rows * cols, bytes_accessed=channels * rows * cols * 8, transcendentals=0
        ),
        name="main",
    )(*held, *recv, *take, *local, lund)


def update_kernel(channel, top, bottom, ah_ref, al_ref, lund_ref, out_in_ref, out_ref, sum_ref):
    target = pl.program_id(1)
    column = channel * (channel + 3) // 2

    def body(t, carry):
        cols = pl.ds(pl.multiple_of(t * TILE, TILE), TILE)
        for half, recv in ((0, top), (1, bottom)):
            rows = slice(half * MAXW, (half + 1) * MAXW)
            value = across(ah_ref, al_ref, half, recv[:, cols])
            if channel == 1:
                sum_ref[rows, cols] = value
            out_ref[0, rows, cols] = out_in_ref[0, rows, cols] + lund_ref[rows, column : column + 1] * value
        return carry

    @pl.when(target == 0)
    def _():
        lax.fori_loop(0, out_ref.shape[2] // TILE, body, 0)

    if channel == 1:

        @pl.when(target == 1)
        def _():
            out_ref[0] = out_in_ref[0] + lund_ref[:, 4:5] * sum_ref[...]


def update(out, arrived, take, lund, channel, first):
    channels, rows, _ = out.shape
    size, width = arrived[0].shape
    step = min(4 * TILE if channel == 1 else 2 * TILE, width)
    block = pl.BlockSpec((1, rows, step), lambda t, k: (channel + k, 0, t + first // step))
    return pl.pallas_call(
        functools.partial(update_kernel, channel),
        grid=(width // step, channels - channel),
        in_specs=[pl.BlockSpec((size, step), lambda t, k: (0, t))] * 2
        + [whole(array) for array in (*take, lund)]
        + [block],
        out_specs=block,
        out_shape=jax.ShapeDtypeStruct(out.shape, out.dtype),
        scratch_shapes=[pltpu.VMEM((rows, step), jnp.float32)],
        input_output_aliases={5: 0},
        compiler_params=ROOM,
        cost_estimate=pl.CostEstimate(
            flops=6 * rows * size * width, bytes_accessed=rows * width * 8 + size * width * 8, transcendentals=0
        ),
        name="update",
    )(*arrived, *take, lund, out)


def ring(axis):
    count = lax.axis_size(axis)
    forward = [(i, (i + 1) % count) for i in range(count)]
    return forward, [(target, source) for source, target in forward]


def exchange(field):
    forward, backward = ring("span")
    low = lax.ppermute(field[:, :, -REACH:], "span", forward)
    return low, lax.ppermute(field[:, :, :REACH], "span", backward)


def shards(random_field, half_widths, band_pads, span_widths, stresses, mean_flow):
    _, _, cols = random_field.shape
    wall_count = lax.axis_size("wall")
    where = jnp.stack([lax.axis_index("wall"), jnp.int32(wall_count)])
    halo = exchange(random_field[:1])
    give, rows, needed = early_tables(where, band_pads, half_widths)
    rest, needed = lax.optimization_barrier((random_field, needed))
    halos = exchange(rest[1:])
    downward, upward = ring("wall")
    spans = list(zip((0,) + SIZES[:-1], SIZES))
    tables, held, ahead = front(spans, random_field, *halo, None, give, None, 0, 1, where, span_widths)

    def across_edges(pieces):
        arrived = []
        for up, down in pieces:
            bottom = lax.ppermute(up, "wall", upward)
            arrived.append((lax.ppermute(down, "wall", downward), bottom))
        return arrived

    def run(number, *operands):
        return steps(number, *operands)

    def steps(number, field, halos, tables, give, where, rows, stresses, mean_flow, held, ahead):
        span = [(0, SIZES[number])]
        first = across_edges(ahead[: number + 1])
        held, pieces = front(span, field, *halos, tables, give, held, 1, 1)
        second = across_edges(pieces)
        held, pieces = front(span, field, *halos, tables, give, held, 2, 2)
        third = across_edges(pieces[:1]) + across_edges(pieces[1:])
        stress_rows = jnp.pad(jnp.concatenate([stresses, mean_flow[None]], axis=0), ((0, 1), (0, 0)))
        take, local, lund = late_tables(where, rows, stress_rows)
        out = main_filter(held, (first,), take, local, lund)
        out = update(out, second[0], take, lund, 1, 0)
        for k, pair in enumerate(third):
            out = update(out, pair, take, lund, 2, k * (cols // len(third)))
        return out

    operands = (random_field, halos, tables, give, where, rows, stresses, mean_flow, held, ahead)
    if len(SIZES) == 1:
        return run(0, *operands)
    which = sum((needed > size).astype(jnp.int32) for size in SIZES[:-1])
    return lax.switch(which, [functools.partial(run, k) for k in range(len(SIZES))], *operands)


def solution(mesh):
    return jax.shard_map(
        shards,
        mesh=mesh,
        in_specs=(P(None, "wall", "span"), P(), P(), P(), P(None, "wall"), P("wall")),
        out_specs=P(None, "wall", "span"),
        check_vma=False,
    )
```

time: 183 us -> 179 us (0.978)
  waiting for transfers between devices: 54.7 us -> 52 us
    ppermute x5, waiting for transfers between devices: 54.6 us -> 52 us  [across_edges(): arrived.append((lax.ppermute(down, 'wall', downward), bottom))]
    pallas_call x6 -> x7, Pallas kernels: 62 us -> 61.7 us  [the longest x3 38.7 us: front(): pl.pallas_call(functools.partial(front_kernel, build, cuts, spans), grid=...]
  transfers between devices with their start and end apart: 14 -> 14, of which waited for: 2 -> 1; matrix products, arithmetic and copies ran while one was open for 2% -> 2% of each run, Pallas kernels for 39% -> 41%
where the time goes in v1:
time: 179 us; the launch traced here: 178 us
  Pallas kernels  88.7 us (50%)
  waiting for transfers between devices  52 us (29%)
  starting transfers between devices  27.3 us (15%)
  local copies, waits for them, and re-layouts  7.57 us (4%)
    ppermute x5, waiting for transfers between devices, across_edges(): arrived.append((lax.ppermute(down, 'wall', downward), bottom))  52 us
    pallas_call x3, Pallas kernels, front(): pl.pallas_call(functools.partial(front_kernel, build, cuts, spans), grid=...  38.7 us
    pallas_call x1, Pallas kernels, main_filter(): pl.pallas_call(functools.partial(main_kernel, counts), grid=(cols // step...  23.4 us
    pallas_call x3, Pallas kernels, update(): pl.pallas_call(functools.partial(update_kernel, channel), grid=(width //...  19.6 us
    ppermute x5, starting transfers between devices, across_edges(): bottom = lax.ppermute(up, 'wall', upward)  12.2 us
    ppermute x2, starting transfers between devices, exchange(): return (low, lax.ppermute(field[:, :, :REACH], 'span', backward))  11.2 us
    ppermute x5, starting transfers between devices, across_edges(): arrived.append((lax.ppermute(down, 'wall', downward), bottom))  3.91 us
    pallas_call x1, Pallas kernels, late_tables(): pl.pallas_call(late_kernel, grid=(2,), in_specs=[pl.BlockSpec(memory_spac...  3.63 us
  transfers between devices with their start and end apart: 14, of which 1 were waited for; matrix products, arithmetic and copies ran while one was open for 2% of the time, Pallas kernels for 41%

profile of v1, /device:TPU:0, one launch (start us, length us, event | category | flops | bytes accessed | tf_op | source)
XLA Modules:
  0.0 177.8 jit_solution(12658362728616803288)
XLA Ops:
  0.0 1.1 fusion
  1.1 6.1 %collective-permute-start.33 = (f32[1,512,128]{2,1,0:T(8,128)S(1)}, f32[1,512,128]{2,1,0:T(8,128)S(1)}, u32[]{:S(2)}, u32[]{:S(2)}) collective-permute-start(f32[1,512,128]{2,1,0:T(8,128)S(1)} %get-tuple-element.240), channel_id=1, source_target_pairs={{4,0},{8,4},{12,8},{16,12},{20,16},{24,20},{28,24},{32,28},{36,32}... | collective-permute-start | bytes 786440 | tf_op jit(solution)/shard_map/ppermute | solution.py:425
  7.3 3.4 %early.1 = (bf16[2,256,256]{2,1,0:T(8,128)(2,1)S(1)}, bf16[2,256,256]{2,1,0:T(8,128)(2,1)S(1)}, f32[128,256]{1,0:T(8,128)S(1)}, s32[1,1]{1,0:T(1,128)}) custom-call(s32[2]{0:T(128)S(1)} %pad_add_fusion.where_ref.refs_0_, s32[32]{0:T(128)} %pads_ref.1, s32[16,128]{1,0:T(8,128)} %bitcast.9), custom_call_target="tpu_custom_call" | custom-call | tf_op jit(solution)/shard_map/early/pallas_call | solution.py:127
  10.6 2.2 %fusion.1 = (f32[2,512,128]{2,1,0:T(8,128)}, f32[2,512,128]{2,1,0:T(8,128)}) fusion(f32[3,512,2048]{2,1,0:T(8,128)} %refs_2_.1), kind=kLoop, calls=%fused_computation.8 | loop fusion | bytes 2097152 | tf_op jit(solution)/shard_map/slice | solution.py:425
  12.9 5.1 %collective-permute-start.31 = (f32[2,512,128]{2,1,0:T(8,128)}, f32[2,512,128]{2,1,0:T(8,128)S(1)}, u32[]{:S(2)}, u32[]{:S(2)}) collective-permute-start(f32[2,512,128]{2,1,0:T(8,128)} %get-tuple-element.242), channel_id=1, source_target_pairs={{4,0},{8,4},{12,8},{16,12},{20,16},{24,20},{28,24},{32,28},{36,32}... | collective-permute-start | bytes 1572872 | tf_op jit(solution)/shard_map/ppermute | solution.py:425
  19.9 14.0 %front.13 = (bf16[8,384,128]{2,1,0:T(8,128)(2,1)S(1)}, bf16[8,384,128]{2,1,0:T(8,128)(2,1)S(1)}, bf16[3,512,2048]{2,1,0:T(8,128)(2,1)}, bf16[3,512,2048]{2,1,0:T...) custom-call(s32[2]{0:T(128)S(1)} %pad_add_fusion.where_ref.refs_0_, ...), custom_call_target="tpu_custom_call" | custom-call | flops 4831838208 | bytes 12582912 | tf_op jit(solution)/shard_map/front/pallas_call | solution.py:291
  34.0 143.8 %conditional.1 = (f32[3,512,2048]{2,1,0:T(8,128)}) conditional(s32[]{:T(128)} %clamp.3, (f32[3,512,2048]{2,1,0:T(8,128)}, f32[2,512,128]{2,1,0:T(8,128)S(1)}, f32[2,512,128]{2,1,0:T(8,128)S(1)}, bf16[2,256,256]{2,1,0:T(8,128)(2,1)S(1)}, bf16[2,256,256]{2,1,0:T(8,128)(2,1)S(1)}, /*index=5*/bf16[8,384,128]{2,1,0:T(8,128)(2,1)S(1)}, ...), branch_computations={%region_0.1_spmd, %region_1.2_spmd, %region_2.3_spmd} | conditional | flops 22548594688 | bytes 142637664 | solution.py:469
  34.2 12.3 %front.9 = (bf16[3,512,2048]{2,1,0:T(8,128)(2,1)}, bf16[3,512,2048]{2,1,0:T(8,128)(2,1)}, f32[184,2048]{1,0:T(8,128)}, f32[184,2048]{1,0:T(8,128)}) custom-call(f32[3,512,2048]{2,1,0:T(8,128)} %get-tuple-element.141.refs_0_, f32[2,512,128]{2,1,0:T(8,128)S(1)} %get-tuple-element.142.refs_1_, ...), custom_call_target="tpu_custom_call", output_to_operand_aliasing={{0}: (7, {}), {1}: (8, {})} | custom-call | flops 4378853376 | bytes 11403264 | tf_op jit(solution)/shard_map/cond/branch_1_fun/front/pallas_call | solution.py:291
  46.5 1.6 collective-permute-start.12
  48.1 1.5 collective-permute-start.14
  49.6 1.7 collective-permute-start.15
  51.6 2.9 %collective-permute-start.13 = (f32[184,2048]{1,0:T(8,128)}, f32[184,2048]{1,0:T(8,128)}, u32[]{:S(2)}, u32[]{:S(2)}) collective-permute-start(f32[184,2048]{1,0:T(8,128)} %get-tuple-element.164), channel_id=1, source_target_pairs={{1,0},{2,1},{3,2},{0,3},{5,4},{6,5},{7,6},{4,7},{9,8},{10,9},{11,1... | collective-permute-start | bytes 4521992 | tf_op jit(solution)/shard_map/cond/branch_1_fun/ppermute | solution.py:443
  55.1 3.6 %late.4 = (bf16[2,256,256]{2,1,0:T(8,128)(2,1)}, bf16[2,256,256]{2,1,0:T(8,128)(2,1)}, bf16[512,512]{1,0:T(8,128)(2,1)}, bf16[512,512]{1,0:T(8,128)(2,1)}, f32[512,128]{1,0:T(8,128)}) custom-call(s32[2]{0:T(128)S(1)} %get-tuple-element.154.where_ref, f32[128,256]{1,0:T(8,128)S(1)} %get-tuple-element.155.rows_ref, f32[8,512]{1,0:T(8,128)} %select_maximum_fusion.1.stress_ref), custom_call_target="tpu_custom_call" | custom-call | tf_op jit(solution)/shard_map/cond/branch_1_fun/late/pallas_call | solution.py:179
  58.8 52.0 %collective-permute-done.16.rest_2_ = f32[32,2048]{1,0:T(8,128)} collective-permute-done((f32[32,2048]{1,0:T(8,128)}, f32[32,2048]{1,0:T(8,128)}, u32[]{:S(2)}, u32[]{:S(2)}) %collective-permute-start.16) | collective-permute-done | bytes 262176 | tf_op jit(solution)/shard_map/cond/branch_1_fun/ppermute | solution.py:444
  110.8 1.5 collective-permute-start.17
  112.3 12.3 %front.10 = (bf16[3,512,2048]{2,1,0:T(8,128)(2,1)}, bf16[3,512,2048]{2,1,0:T(8,128)(2,1)}, f32[184,1024]{1,0:T(8,128)}, f32[184,1024]{1,0:T(8,128)}, f32[184,1024]{1,0:T(8,128)}, /*index=5*/f32[184,1024]{1,0:T(8,128)}) custom-call(f32[3,512,2048]{2,1,0:T(8,128)} %get-tuple-element.141.refs_0_, ...), custom_call_target="tpu_custom_call", output_to_operand_aliasing={{0}: (7, {}), {1}: (8, {})} | custom-call | flops 4378853376 | bytes 11403264 | tf_op jit(solution)/shard_map/cond/branch_1_fun/front/pallas_call | solution.py:291
  125.2 2.7 %collective-permute-start.9 = (f32[184,1024]{1,0:T(8,128)}, f32[184,1024]{1,0:T(8,128)S(1)}, u32[]{:S(2)}, u32[]{:S(2)}) collective-permute-start(f32[184,1024]{1,0:T(8,128)} %get-tuple-element.153), channel_id=1, source_target_pairs={{1,0},{2,1},{3,2},{0,3},{5,4},{6,5},{7,6},{4,7},{9,8},{10,9},{11,1... | collective-permute-start | bytes 2261000 | tf_op jit(solution)/shard_map/cond/branch_1_fun/ppermute | solution.py:443
  128.0 3.2 %collective-permute-start.11 = (f32[184,1024]{1,0:T(8,128)}, f32[184,1024]{1,0:T(8,128)S(1)}, u32[]{:S(2)}, u32[]{:S(2)}) collective-permute-start(f32[184,1024]{1,0:T(8,128)} %get-tuple-element.162), channel_id=1, source_target_pairs={{1,0},{2,1},{3,2},{0,3},{5,4},{6,5},{7,6},{4,7},{9,8},{10,9},{11,1... | collective-permute-start | bytes 2261000 | tf_op jit(solution)/shard_map/cond/branch_1_fun/ppermute | solution.py:443
  131.2 23.4 %main.4.out_in_ref = f32[3,512,2048]{2,1,0:T(8,128)} custom-call(bf16[3,512,2048]{2,1,0:T(8,128)(2,1)} %get-tuple-element.165.sh_ref, bf16[3,512,2048]{2,1,0:T(8,128)(2,1)} %get-tuple-element.166.sl_ref, f32[152,2048]{1,0:T(8,128)} %collective-permute-done.14.rest_0_, f32[152,2048]{1,0:T(8,128)} %collective-permute-done.15.rest_1_, ...), custom_call_target="tpu_custom_call" | custom-call | flops 9663676416 | bytes 25165824 | tf_op jit(solution)/shard_map/cond/branch_1_fun/main/pallas_call | solution.py:352
  154.6 11.0 %update.12.out_in_ref = f32[3,512,2048]{2,1,0:T(8,128)} custom-call(f32[184,2048]{1,0:T(8,128)} %collective-permute-done.12.top, f32[184,2048]{1,0:T(8,128)} %collective-permute-done.13.bottom, bf16[2,256,256]{2,1,0:T(8,128)(2,1)} %get-tuple-element.158.rest_4_.ah_ref, ...), custom_call_target="tpu_custom_call", output_to_operand_aliasing={{}: (5, {})} | custom-call | flops 1157627904 | bytes 11403264 | tf_op jit(solution)/shard_map/cond/branch_1_fun/update/pallas_call | solution.py:398
  166.6 0.9 copy-done.7
  167.4 4.3 %update.13.out_in_ref = f32[3,512,2048]{2,1,0:T(8,128)} custom-call(f32[184,1024]{1,0:T(8,128)} %copy-done.6, f32[184,1024]{1,0:T(8,128)} %copy-done.7, bf16[2,256,256]{2,1,0:T(8,128)(2,1)} %get-tuple-element.158.rest_4_.ah_ref, bf16[2,256,256]{2,1,0:T(8,128)(2,1)} %get-tuple-element.159.rest_5_.al_ref, ...), custom_call_target="tpu_custom_call", output_to_operand_aliasing={{}: (5, {})} | custom-call | flops 578813952 | bytes 5701632 | tf_op jit(solution)/shard_map/cond/branch_1_fun/update/pallas_call | solution.py:398
  172.6 0.9 copy-done.5
  173.5 4.3 %update.14 = f32[3,512,2048]{2,1,0:T(8,128)} custom-call(f32[184,1024]{1,0:T(8,128)} %copy-done.4, f32[184,1024]{1,0:T(8,128)} %copy-done.5, bf16[2,256,256]{2,1,0:T(8,128)(2,1)} %get-tuple-element.158.rest_4_.ah_ref, bf16[2,256,256]{2,1,0:T(8,128)(2,1)} %get-tuple-element.159.rest_5_.al_ref, ...), custom_call_target="tpu_custom_call", output_to_operand_aliasing={{}: (5, {})} | custom-call | flops 578813952 | bytes 5701632 | tf_op jit(solution)/shard_map/cond/branch_1_fun/update/pallas_call | solution.py:398
  (36 shorter events, 4.1 us)
Async XLA Ops:
  1.1 18.0 %collective-permute-start.33 = (f32[1,512,128]{2,1,0:T(8,128)S(1)}, f32[1,512,128]{2,1,0:T(8,128)S(1)}, u32[]{:S(2)}, u32[]{:S(2)}) collective-permute-start(f32[1,512,128]{2,1,0:T(8,128)S(1)} %get-tuple-element.240), channel_id=1, source_target_pairs={{4,0},{8,4},{12,8},{16,12},{20,16},{24,20},{28,24},{32,28},{36,32}... | collective-permute-start | bytes 786440 | tf_op jit(solution)/shard_map/ppermute | solution.py:425
  7.2 11.9 %collective-permute-start.32 = (f32[1,512,128]{2,1,0:T(8,128)S(1)}, f32[1,512,128]{2,1,0:T(8,128)S(1)}, u32[]{:S(2)}, u32[]{:S(2)}) collective-permute-start(f32[1,512,128]{2,1,0:T(8,128)S(1)} %get-tuple-element.241), channel_id=1, source_target_pairs={{0,4},{4,8},{8,12},{12,16},{16,20},{20,24},{24,28},{28,32},{32,36}... | collective-permute-start | bytes 786440 | tf_op jit(solution)/shard_map/ppermute | solution.py:424
  12.9 21.1 %collective-permute-start.31 = (f32[2,512,128]{2,1,0:T(8,128)}, f32[2,512,128]{2,1,0:T(8,128)S(1)}, u32[]{:S(2)}, u32[]{:S(2)}) collective-permute-start(f32[2,512,128]{2,1,0:T(8,128)} %get-tuple-element.242), channel_id=1, source_target_pairs={{4,0},{8,4},{12,8},{16,12},{20,16},{24,20},{28,24},{32,28},{36,32}... | collective-permute-start | bytes 1572872 | tf_op jit(solution)/shard_map/ppermute | solution.py:425
  17.9 16.0 %collective-permute-start.30 = (f32[2,512,128]{2,1,0:T(8,128)}, f32[2,512,128]{2,1,0:T(8,128)S(1)}, u32[]{:S(2)}, u32[]{:S(2)}) collective-permute-start(f32[2,512,128]{2,1,0:T(8,128)} %get-tuple-element.243), channel_id=1, source_target_pairs={{0,4},{4,8},{8,12},{12,16},{16,20},{20,24},{24,28},{28,32},{32,36}... | collective-permute-start | bytes 1572872 | tf_op jit(solution)/shard_map/ppermute | solution.py:424
  19.1 0.7 copy-start.14
  19.1 0.8 copy-start.15
  19.9 14.0 %copy-start.12 = (f32[6,512]{1,0:T(8,128)S(1)}, f32[6,512]{1,0:T(8,128)}, u32[]{:S(2)}) copy-start(f32[6,512]{1,0:T(8,128)} %param.13) | copy-start | bytes 36868
  19.9 14.1 %copy-start.13 = (f32[512]{0:T(512)S(1)}, f32[512]{0:T(512)}, u32[]{:S(2)}) copy-start(f32[512]{0:T(512)} %param.14) | copy-start | bytes 6148
  46.5 81.5 %collective-permute-start.12 = (f32[184,2048]{1,0:T(8,128)}, f32[184,2048]{1,0:T(8,128)}, u32[]{:S(2)}, u32[]{:S(2)}) collective-permute-start(f32[184,2048]{1,0:T(8,128)} %get-tuple-element.163), channel_id=1, source_target_pairs={{0,1},{1,2},{2,3},{3,0},{4,5},{5,6},{6,7},{7,4},{8,9},{9,10},{10,1... | collective-permute-start | bytes 4521992 | tf_op jit(solution)/shard_map/cond/branch_1_fun/ppermute | solution.py:444
  48.1 77.2 %collective-permute-start.14 = (f32[152,2048]{1,0:T(8,128)}, f32[152,2048]{1,0:T(8,128)}, u32[]{:S(2)}, u32[]{:S(2)}) collective-permute-start(f32[152,2048]{1,0:T(8,128)} %get-tuple-element.167), channel_id=1, source_target_pairs={{0,1},{1,2},{2,3},{3,0},{4,5},{5,6},{6,7},{7,4},{8,9},{9,10},{10,1... | collective-permute-start | bytes 3735560 | tf_op jit(solution)/shard_map/cond/branch_1_fun/ppermute | solution.py:444
  49.6 78.4 %collective-permute-start.15 = (f32[152,2048]{1,0:T(8,128)}, f32[152,2048]{1,0:T(8,128)}, u32[]{:S(2)}, u32[]{:S(2)}) collective-permute-start(f32[152,2048]{1,0:T(8,128)} %get-tuple-element.168), channel_id=1, source_target_pairs={{1,0},{2,1},{3,2},{0,3},{5,4},{6,5},{7,6},{4,7},{9,8},{10,9},{11,1... | collective-permute-start | bytes 3735560 | tf_op jit(solution)/shard_map/cond/branch_1_fun/ppermute | solution.py:443
  51.3 59.5 %collective-permute-start.16 = (f32[32,2048]{1,0:T(8,128)}, f32[32,2048]{1,0:T(8,128)}, u32[]{:S(2)}, u32[]{:S(2)}) collective-permute-start(f32[32,2048]{1,0:T(8,128)} %get-tuple-element.169), channel_id=1, source_target_pairs={{0,1},{1,2},{2,3},{3,0},{4,5},{5,6},{6,7},{7,4},{8,9},{9,10},{10,1... | collective-permute-start | bytes 786440 | tf_op jit(solution)/shard_map/cond/branch_1_fun/ppermute | solution.py:444
  51.6 103.0 %collective-permute-start.13 = (f32[184,2048]{1,0:T(8,128)}, f32[184,2048]{1,0:T(8,128)}, u32[]{:S(2)}, u32[]{:S(2)}) collective-permute-start(f32[184,2048]{1,0:T(8,128)} %get-tuple-element.164), channel_id=1, source_target_pairs={{1,0},{2,1},{3,2},{0,3},{5,4},{6,5},{7,6},{4,7},{9,8},{10,9},{11,1... | collective-permute-start | bytes 4521992 | tf_op jit(solution)/shard_map/cond/branch_1_fun/ppermute | solution.py:443
  110.8 13.9 %collective-permute-start.17 = (f32[32,2048]{1,0:T(8,128)}, f32[32,2048]{1,0:T(8,128)S(1)}, u32[]{:S(2)}, u32[]{:S(2)}) collective-permute-start(f32[32,2048]{1,0:T(8,128)} %get-tuple-element.170), channel_id=1, source_target_pairs={{1,0},{2,1},{3,2},{0,3},{5,4},{6,5},{7,6},{4,7},{9,8},{10,9},{11,1... | collective-permute-start | bytes 786440 | tf_op jit(solution)/shard_map/cond/branch_1_fun/ppermute | solution.py:443
  124.6 6.6 %copy-start.16 = (f32[32,2048]{1,0:T(8,128)}, f32[32,2048]{1,0:T(8,128)S(1)}, u32[]{:S(2)}) copy-start(f32[32,2048]{1,0:T(8,128)S(1)} %collective-permute-done.17.rest_3_) | copy-start | bytes 786436 | tf_op jit(solution)/shard_map/cond
  124.6 47.1 %collective-permute-start.8 = (f32[184,1024]{1,0:T(8,128)}, f32[184,1024]{1,0:T(8,128)S(1)}, u32[]{:S(2)}, u32[]{:S(2)}) collective-permute-start(f32[184,1024]{1,0:T(8,128)} %get-tuple-element.152), channel_id=1, source_target_pairs={{0,1},{1,2},{2,3},{3,0},{4,5},{5,6},{6,7},{7,4},{8,9},{9,10},{10,1... | collective-permute-start | bytes 2261000 | tf_op jit(solution)/shard_map/cond/branch_1_fun/ppermute | solution.py:444
  125.2 46.5 %collective-permute-start.9 = (f32[184,1024]{1,0:T(8,128)}, f32[184,1024]{1,0:T(8,128)S(1)}, u32[]{:S(2)}, u32[]{:S(2)}) collective-permute-start(f32[184,1024]{1,0:T(8,128)} %get-tuple-element.153), channel_id=1, source_target_pairs={{1,0},{2,1},{3,2},{0,3},{5,4},{6,5},{7,6},{4,7},{9,8},{10,9},{11,1... | collective-permute-start | bytes 2261000 | tf_op jit(solution)/shard_map/cond/branch_1_fun/ppermute | solution.py:443
  128.0 37.7 %collective-permute-start.10 = (f32[184,1024]{1,0:T(8,128)}, f32[184,1024]{1,0:T(8,128)S(1)}, u32[]{:S(2)}, u32[]{:S(2)}) collective-permute-start(f32[184,1024]{1,0:T(8,128)} %get-tuple-element.161), channel_id=1, source_target_pairs={{0,1},{1,2},{2,3},{3,0},{4,5},{5,6},{6,7},{7,4},{8,9},{9,10},{10,1... | collective-permute-start | bytes 2261000 | tf_op jit(solution)/shard_map/cond/branch_1_fun/ppermute | solution.py:444
  128.0 37.7 %collective-permute-start.11 = (f32[184,1024]{1,0:T(8,128)}, f32[184,1024]{1,0:T(8,128)S(1)}, u32[]{:S(2)}, u32[]{:S(2)}) collective-permute-start(f32[184,1024]{1,0:T(8,128)} %get-tuple-element.162), channel_id=1, source_target_pairs={{1,0},{2,1},{3,2},{0,3},{5,4},{6,5},{7,6},{4,7},{9,8},{10,9},{11,1... | collective-permute-start | bytes 2261000 | tf_op jit(solution)/shard_map/cond/branch_1_fun/ppermute | solution.py:443
  165.7 0.9 copy-start.6
  166.6 0.9 copy-start.7
  171.7 0.9 copy-start.4
  172.6 0.9 copy-start.5
